TPU v7x, 32 devices: a 4x2x2 block of a 4x4x8 slice. The times are simulated.
32 devices in a mesh: dp: 4 (over y, z), ep: 8 (over x, core).
Axes of the slice: x: 4, y: 2, z: 2, core: 2. Of those that a mesh axis runs over, the one named last changes fastest.
The devices are a block of a 4x4x8 slice.
Arguments:
- x: bfloat16 [96, 128, 2048], P(('dp', 'ep')), parts along dimension 0
- idx: int32 [96, 128, 8], P(('dp', 'ep')), parts along dimension 0
- gates: float32 [96, 128, 8], P(('dp', 'ep')), parts along dimension 0
- g1: float32 [2048], replicated
- wq: bfloat16 [2048, 4096], replicated
- wk: bfloat16 [2048, 4096], replicated
- wv: bfloat16 [2048, 4096], replicated
- wo: bfloat16 [4096, 2048], replicated
- g2: float32 [2048], replicated
- w1: bfloat16 [128, 2048, 768], P('ep')
- w3: bfloat16 [128, 2048, 768], P('ep')
- w2: bfloat16 [128, 768, 2048], P('ep')
Outputs:
- output: bfloat16 [96, 128, 2048], P(('dp', 'ep')), parts along dimension 0
There are 4 independent parts. A program takes and returns all parts, laid end to end along the dimension named above; an argument that names none is the same for every part.
All inputs are finite; a program needn't handle non-finite values.
Results may differ from a plain program's by a relative error of at most 0.0130551.
Values are sent between devices in bfloat16 or wider.
A program may use at most 768 MiB of HBM per device.

v0:
```python
import jax
import jax.numpy as jnp
from jax import lax
from jax.sharding import PartitionSpec as P

EPS = 1e-6
HEAD = 128


def rms(x, g):
    xf = x.astype(jnp.float32)
    return (xf * lax.rsqrt(jnp.mean(xf * xf, axis=-1, keepdims=True) + EPS) * g).astype(jnp.bfloat16)


def attend(q, k, v):
    n = q.shape[0]
    s = jnp.einsum('qhd,khd->hqk', q, k, preferred_element_type=jnp.float32) * q.shape[-1] ** -0.5
    mask = jnp.arange(n)[:, None] >= jnp.arange(n)[None, :]
    s = jnp.where(mask[None], s, -1e30)
    p = jax.nn.softmax(s, axis=-1).astype(jnp.bfloat16)
    return jnp.einsum('hqk,khd->qhd', p, v, preferred_element_type=jnp.float32).astype(jnp.bfloat16)


def slot_pos(flat, n_exp):
    n = flat.shape[0]
    order = jnp.argsort(flat, stable=True)
    se = flat[order]
    counts = jnp.zeros((n_exp,), jnp.int32).at[flat].add(1)
    starts = jnp.cumsum(counts) - counts
    ps = jnp.arange(n, dtype=jnp.int32) - starts[se]
    return jnp.zeros((n,), jnp.int32).at[order].set(ps)


def solution(mesh):
    ep = mesh.shape['ep']
    tok = P(('dp', 'ep'))
    rep = P()
    exs = P('ep')

    def body(x, idx, gates, g1, wq, wk, wv, wo, g2, w1, w3, w2):
        n, s_len, d = x.shape
        t = n * s_len
        top = idx.shape[-1]
        g_loc = w1.shape[0]
        n_exp = g_loc * ep
        avg = top * t // n_exp
        cap = avg + avg // 2
        heads = wq.shape[1] // HEAD
        xf = x.reshape(t, d)
        xn = rms(xf, g1)

        def proj(w):
            return jnp.dot(xn, w, preferred_element_type=jnp.float32).astype(jnp.bfloat16).reshape(n, s_len, heads, HEAD)

        q = proj(wq)
        k = proj(wk)
        v = proj(wv)
        o = lax.map(lambda a: attend(a[0], a[1], a[2]), (q, k, v))
        att = jnp.dot(o.reshape(t, heads * HEAD), wo, preferred_element_type=jnp.float32).astype(jnp.bfloat16)
        h = (xf.astype(jnp.float32) + att.astype(jnp.float32)).astype(jnp.bfloat16)
        z = rms(h, g2)
        flat = idx.reshape(t * top)
        dest = flat * cap + slot_pos(flat, n_exp)
        buf = jnp.zeros((n_exp * cap, d), jnp.bfloat16).at[dest].set(jnp.repeat(z, top, axis=0))
        recv = lax.all_to_all(buf, 'ep', 0, 0, tiled=True)
        r = recv.reshape(ep, g_loc, cap, d).transpose(1, 0, 2, 3).reshape(g_loc, ep * cap, d)
        h1 = jnp.einsum('gnd,gdf->gnf', r, w1, preferred_element_type=jnp.float32)
        h3 = jnp.einsum('gnd,gdf->gnf', r, w3, preferred_element_type=jnp.float32)
        u = (jax.nn.silu(h1) * h3).astype(jnp.bfloat16)
        e_out = jnp.einsum('gnf,gfd->gnd', u, w2, preferred_element_type=jnp.float32).astype(jnp.bfloat16)
        e_out = e_out.reshape(g_loc, ep, cap, d).transpose(1, 0, 2, 3).reshape(ep * g_loc * cap, d)
        back = lax.all_to_all(e_out, 'ep', 0, 0, tiled=True)
        got = back[dest].reshape(t, top, d).astype(jnp.float32)
        moe = jnp.sum(got * gates.reshape(t, top, 1), axis=1)
        y = (h.astype(jnp.float32) + moe).astype(jnp.bfloat16)
        return y.reshape(n, s_len, d)

    return jax.shard_map(body, mesh=mesh, in_specs=(tok, tok, tok, rep, rep, rep, rep, rep, rep, exs, exs, exs), out_specs=tok, check_vma=False)
```

profile of v0, /device:TPU:81, one launch (start us, length us, event | category | flops | bytes accessed | tf_op | source)
XLA Modules:
  0.0 886.5 jit_solution(2752881229576887406)
XLA Ops:
  0.0 0.8 copy.53
  0.8 0.1 reshape.159
  1.0 0.1 reshape.160
  1.1 5.8 sort.17
  6.9 17.4 %gather_fusion = s32[3072]{0:T(1024)S(1)} fusion(s32[3072]{0:T(1024)S(1)} %reshape.159, s32[3072]{0:T(1024)S(1)} %get-tuple-element.69), kind=kCustom, calls=%fused_computation | custom fusion | bytes 36864 | tf_op jit(solution)/shard_map/gather | solution.py:27
  24.4 21.7 %scatter_custom_fusion = s32[128]{0:T(128)S(1)} fusion(s32[3072]{0:T(1024)S(1)} %bitcast.120, s32[3072]{0:T(1024)S(1)} %broadcast.102, s32[]{:T(128)} %copy.130), kind=kCustom, calls=%fused_computation.80 | custom fusion | flops 3072 | bytes 516 | tf_op jit(solution)/shard_map/scatter-add | solution.py:28
  46.1 0.1 copy.55
  46.2 0.2 reduce-window.9
  46.4 0.1 reduce.1
  46.5 18.7 %gather_fusion.1 = s32[3072]{0:T(1024)S(1)} fusion(s32[128]{0:T(128)S(1)} %sub.14, s32[3072]{0:T(1024)S(1)} %broadcast_clamp_fusion.1), kind=kCustom, calls=%fused_computation.1 | custom fusion | bytes 36864 | tf_op jit(solution)/shard_map/gather | solution.py:30
  65.2 12.0 %scatter_custom_fusion.1 = s32[3072]{0:T(1024)S(1)} fusion(s32[3072]{0:T(1024)S(1)} %get-tuple-element.70, s32[3072]{0:T(1024)S(1)} %iota_subtract_fusion, s32[]{:T(128)} %copy.130), kind=kCustom, calls=%fused_computation.76 | custom fusion | bytes 12292 | tf_op jit(solution)/shard_map/scatter | solution.py:31
  77.2 0.6 broadcast_clamp_fusion
  77.8 0.4 fusion.37
  78.2 0.4 fusion.39
  78.7 10.5 %fusion.46 = bf16[48,8,32,128]{3,1,2,0:T(8,128)(2,1)S(1)} fusion(bf16[384,2048]{1,0:T(8,128)(2,1)S(1)} %fusion.39, bf16[2048,4096]{1,0:T(8,128)(2,1)} %param.20), kind=kOutput, calls=%fused_computation.65 | convolution fusion | flops 6444023808 | bytes 21495808 | tf_op jit(solution)/shard_map/dot_general | solution.py:53
  89.3 2.5 copy.70
  91.8 7.0 fusion.47
  98.8 2.6 copy.71
  101.4 10.3 %fusion.48 = bf16[48,8,32,128]{3,1,2,0:T(8,128)(2,1)S(1)} fusion(bf16[384,2048]{1,0:T(8,128)(2,1)S(1)} %fusion.39, bf16[2048,4096]{1,0:T(8,128)(2,1)} %param.19), kind=kOutput, calls=%fused_computation.67 | convolution fusion | flops 6444023808 | bytes 21495808 | tf_op jit(solution)/shard_map/dot_general | solution.py:53
  111.7 2.6 copy.72
  114.3 36.4 %while.10 = (s32[]{:T(128)}, bf16[3,128,32,128]{3,2,1,0:T(8,128)(2,1)}, bf16[3,128,32,128]{3,2,1,0:T(8,128)(2,1)}, bf16[3,128,32,128]{3,2,1,0:T(8,128)(2,1)}, bf16[3,128,32,128]{3,2,1,0:T(8,128)(2,1)}, /*index=5*/s32[]{:T(128)}) while((s32[]{:T(128)}, bf16[3,128,32,128]{3,2,1,0:T(8,128)(2,1)}, bf16[3,128,32,128]{3,2,1,0:T(8,128)(2,1)}, ...), condition=%wide.region_4.5_spmd, body=%wide.region_1.4_spmd.sunk | while | flops 407916800 | bytes 23151180 | solution.py:58
  114.5 1.9 constant_dynamic-slice_fusion.6
  116.4 1.3 fusion.78
  117.7 2.1 fusion.79
  119.9 1.3 constant_dynamic-slice_fusion.5
  121.1 1.0 copy.121
  122.1 2.4 fusion.80
  124.5 1.0 copy.122
  125.5 1.0 constant_dynamic-update-slice_fusion.2
  126.6 1.9 constant_dynamic-slice_fusion.6
  128.5 1.3 fusion.78
  129.7 2.1 fusion.79
  131.9 1.3 constant_dynamic-slice_fusion.5
  133.2 1.0 copy.121
  134.2 2.4 fusion.80
  136.6 1.0 copy.122
  137.5 1.1 constant_dynamic-update-slice_fusion.2
  138.6 1.9 constant_dynamic-slice_fusion.6
  140.5 1.3 fusion.78
  141.8 2.1 fusion.79
  143.9 1.3 constant_dynamic-slice_fusion.5
  145.2 1.0 copy.121
  146.2 2.4 fusion.80
  148.6 1.0 copy.122
  149.6 1.0 constant_dynamic-update-slice_fusion.2
  150.6 12.2 %fusion.30 = (f32[384]{0:T(512)S(1)}, bf16[384,2048]{1,0:T(8,128)(2,1)S(1)}) fusion(bf16[4096,2048]{1,0:T(8,128)(2,1)} %param.21, bf16[48,8,32,128]{3,2,1,0:T(8,128)(2,1)} %bitcast.124, bf16[3,128,2048]{2,1,0:T(8,128)(2,1)} %param.14), kind=kOutput, calls=%fused_computation.50 | convolution fusion | flops 6448741888 | bytes 23070208 | tf_op jit(solution)/shard_map/dot_general | solution.py:59
  162.9 1.1 copy-done.1
  164.0 0.4 fusion.32
  164.4 28.5 %scatter_custom_fusion.2 = bf16[4608,2048]{1,0:T(8,128)(2,1)} fusion(s32[3072]{0:T(1024)S(1)} %get-tuple-element.66, bf16[]{:T(256)} %constant.10.clone.1, bf16[384,2048]{1,0:T(8,128)(2,1)S(1)} %fusion.32), kind=kCustom, calls=%fused_computation.39 | custom fusion | bytes 20447234 | tf_op jit(solution)/shard_map/scatter | solution.py:64
  192.9 212.3 %all_to_all.21 = bf16[8,576,2048]{2,1,0:T(8,128)(2,1)S(1)} all-to-all(bf16[8,576,2048]{2,1,0:T(8,128)(2,1)} %bitcast.108), channel_id=1, replica_groups=mesh['dp'=4,'ep'=8] {'ep'}, dimensions={0} | all-to-all | bytes 37748736 | tf_op jit(solution)/shard_map/all_to_all | solution.py:65
  405.2 26.7 %copy.56 = bf16[8,576,2048]{2,0,1:T(8,128)(2,1)S(1)} copy(bf16[8,576,2048]{2,1,0:T(8,128)(2,1)S(1)} %all_to_all.21) | data formatting | bytes 37748736 | tf_op jit(solution)/shard_map/all_to_all | solution.py:65
  432.0 12.0 %copy.57 = bf16[16,8,36,2048]{3,0,2,1:T(8,128)(2,1)} copy(bf16[16,8,36,2048]{3,1,2,0:T(8,128)(2,1)S(1)} %bitcast.109) | data formatting | bytes 37748736 | tf_op jit(solution)/shard_map/transpose | solution.py:66
  443.9 46.5 %fusion.17 = f32[16,288,768]{2,1,0:T(8,128)} fusion(bf16[16,2048,768]{2,1,0:T(8,128)(2,1)} %param.24, bf16[16,288,2048]{2,0,1:T(8,128)(2,1)} %bitcast.115), kind=kOutput, calls=%fused_computation.33 | convolution fusion | flops 14495514624 | bytes 83361792 | tf_op jit(solution)/shard_map/gnd,gdf->gnf/dot_general | solution.py:68
  490.5 53.5 %multiply_convert_fusion.clone.4 = bf16[16,288,768]{2,1,0:T(8,128)(2,1)} fusion(f32[16,288,768]{2,1,0:T(8,128)} %fusion.17, bf16[16,2048,768]{2,1,0:T(8,128)(2,1)} %param.23, bf16[16,288,2048]{2,0,1:T(8,128)(2,1)} %bitcast.116), kind=kOutput, calls=%fused_computation.37.clone.clone.clone.1 | convolution fusion | flops 14516748288 | bytes 90439680 | tf_op jit(solution)/shard_map/gnd,gdf->gnf/dot_general | solution.py:67
  543.9 28.5 %convolution_convert_fusion.1 = bf16[16,288,2048]{2,1,0:T(8,128)(2,1)} fusion(bf16[16,768,2048]{2,1,0:T(8,128)(2,1)} %param.25, bf16[16,288,768]{2,1,0:T(8,128)(2,1)} %multiply_convert_fusion.clone.4), kind=kOutput, calls=%fused_computation.38 | convolution fusion | flops 14504951808 | bytes 76283904 | tf_op jit(solution)/shard_map/gnf,gfd->gnd/dot_general | solution.py:70
  572.4 17.1 %copy.60 = bf16[16,288,2048]{2,0,1:T(8,128)(2,1)S(1)} copy(bf16[16,288,2048]{2,1,0:T(8,128)(2,1)} %convolution_convert_fusion.1) | data formatting | bytes 37748736 | tf_op jit(solution)/shard_map/convert_element_type | solution.py:70
  589.4 25.8 %copy.61 = bf16[8,16,36,2048]{3,0,2,1:T(8,128)(2,1)S(1)} copy(bf16[8,16,36,2048]{3,1,2,0:T(8,128)(2,1)S(1)} %bitcast.110) | data formatting | bytes 37748736 | tf_op jit(solution)/shard_map/transpose | solution.py:71
  615.2 12.0 %copy.62 = bf16[8,576,2048]{2,1,0:T(8,128)(2,1)} copy(bf16[8,576,2048]{2,0,1:T(8,128)(2,1)S(1)} %bitcast.111) | data formatting | bytes 37748736 | tf_op jit(solution)/shard_map/all_to_all | solution.py:72
  627.2 7.0 all-to-all-start.1
  634.2 0.1 copy.63
  634.3 205.8 %all-to-all-done.1 = bf16[8,576,2048]{2,1,0:T(8,128)(2,1)} async-done(((bf16[8,576,2048]{2,1,0:T(8,128)(2,1)}), bf16[8,576,2048]{2,1,0:T(8,128)(2,1)}, u32[]{:S(2)}, u32[]{:S(2)}) %all-to-all-start.1) | async-done | bytes 18874400 | tf_op jit(solution)/shard_map/all_to_all | solution.py:72
  840.1 32.6 %gather_fusion.2 = bf16[3072,2048]{1,0:T(8,128)(2,1)} fusion(bf16[4608,2048]{1,0:T(8,128)(2,1)} %bitcast.19, s32[3072]{0:T(1024)S(1)} %copy-done.3), kind=kCustom, calls=%fused_computation.2 | custom fusion | bytes 25178112 | tf_op jit(solution)/shard_map/gather | solution.py:73
  872.8 11.6 %fusion.16 = f32[384,2048]{1,0:T(8,128)S(1)} fusion(bf16[3072,2048]{1,0:T(8,128)(2,1)} %gather_fusion.2, f32[384,8]{1,0:T(8,128)S(1)} %copy.63), kind=kLoop, calls=%fused_computation.32 | loop fusion | flops 18087936 | bytes 15740928 | tf_op jit(solution)/shard_map/reduce_sum | solution.py:74
  884.4 1.6 fusion.33
  (36 shorter events, 0.2 us)
Async XLA Ops:
  46.5 31.3 %copy-start = (bf16[3,128,2048]{2,1,0:T(8,128)(2,1)S(1)}, bf16[3,128,2048]{2,1,0:T(8,128)(2,1)}, u32[]{:S(2)}) copy-start(bf16[3,128,2048]{2,1,0:T(8,128)(2,1)} %param.14) | copy-start | bytes 4718596
  46.5 31.7 %copy-start.5 = (f32[2048]{0:T(1024)S(1)}, f32[2048]{0:T(1024)}, u32[]{:S(2)}) copy-start(f32[2048]{0:T(1024)} %param.17) | copy-start | bytes 24580
  78.2 13.6 %slice-start = ((s8[16777216]{0:T(1024)(128)(4,1)}), s8[4194304]{0:T(1024)(128)(4,1)S(1)}, s32[]{:S(2)}) async-start(s8[16777216]{0:T(1024)(128)(4,1)} %bitcast.122), calls=%async_computation.2 | async-start | bytes 8388608
  78.7 13.1 %slice-start.1 = ((s8[16777216]{0:T(1024)(128)(4,1)}), s8[4194304]{0:T(1024)(128)(4,1)S(1)}, s32[]{:S(2)}) async-start(s8[16777216]{0:T(1024)(128)(4,1)} %bitcast.122), calls=%async_computation.3 | async-start | bytes 8388608
  78.7 13.1 %slice-start.2 = ((s8[16777216]{0:T(1024)(128)(4,1)}), s8[4194304]{0:T(1024)(128)(4,1)S(1)}, s32[]{:S(2)}) async-start(s8[16777216]{0:T(1024)(128)(4,1)} %bitcast.122), calls=%async_computation.4 | async-start | bytes 8388608
  78.7 13.1 %slice-start.3 = ((s8[16777216]{0:T(1024)(128)(4,1)}), s8[4194304]{0:T(1024)(128)(4,1)S(1)}, s32[]{:S(2)}) async-start(s8[16777216]{0:T(1024)(128)(4,1)} %bitcast.122), calls=%async_computation.5 | async-start | bytes 8388608
  150.6 13.4 %copy-start.6 = (f32[2048]{0:T(1024)S(1)}, f32[2048]{0:T(1024)}, u32[]{:S(2)}) copy-start(f32[2048]{0:T(1024)} %param.22) | copy-start | bytes 24580
  162.8 1.1 copy-start.1
  627.2 7.0 copy-start.4
  627.2 212.9 %copy-start.3 = (s32[3072]{0:T(1024)S(1)}, s32[3072]{0:T(1024)}, u32[]{:S(2)}) copy-start(s32[3072]{0:T(1024)} %get-tuple-element.65) | copy-start | bytes 36868
  627.2 212.9 %all-to-all-start.1 = ((bf16[8,576,2048]{2,1,0:T(8,128)(2,1)}), bf16[8,576,2048]{2,1,0:T(8,128)(2,1)}, u32[]{:S(2)}, u32[]{:S(2)}) async-start(bf16[8,576,2048]{2,1,0:T(8,128)(2,1)} %copy.62), calls=%async_computation.1 | async-start | bytes 37748736 | tf_op jit(solution)/shard_map/all_to_all | solution.py:72
  872.8 11.6 %copy-start.2 = (bf16[384,2048]{1,0:T(8,128)(2,1)S(1)}, bf16[384,2048]{1,0:T(8,128)(2,1)}, u32[]{:S(2)}) copy-start(bf16[384,2048]{1,0:T(8,128)(2,1)} %copy-done.1) | copy-start | bytes 4718596
where the time goes:
time: 891 us; the launch traced here: 886 us
  local copies, waits for them, and re-layouts  231 us (26%)
  blocking collectives  212 us (24%)
  waiting for transfers between devices  206 us (23%)
  matrix products  186 us (21%)
  other arithmetic  42.9 us (5%)
    all_to_all x1, blocking collectives, body(): recv = lax.all_to_all(buf, 'ep', 0, 0, tiled=True)  212 us
    all_to_all x1, waiting for transfers between devices, body(): back = lax.all_to_all(e_out, 'ep', 0, 0, tiled=True)  206 us
    dot_general x1, matrix products, body(): h1 = jnp.einsum('gnd,gdf->gnf', r, w1, preferred_element_type=jnp.float32)  53.5 us
    dot_general x1, matrix products, body(): h3 = jnp.einsum('gnd,gdf->gnf', r, w3, preferred_element_type=jnp.float32)  46.5 us
    gather x1, local copies, waits for them, and re-layouts, body(): got = back[dest].reshape(t, top, d).astype(jnp.float32)  32.6 us
    scatter x1, local copies, waits for them, and re-layouts, body(): jnp.zeros((n_exp * cap, d), jnp.bfloat16).at[dest]  28.5 us
    dot_general x1, matrix products, body(): jnp.einsum('gnf,gfd->gnd', u, w2, preferred_element_type=jnp.float32)  28.5 us
    dot_general x3, matrix products, proj(): jnp.dot(xn, w, preferred_element_type=jnp.float32).astype(jnp.bfloat16)  27.9 us
  transfers between devices with their start and end apart: 1, of which 1 were waited for; matrix products, arithmetic and copies ran while one was open for 0% of the time, Pallas kernels for 0%

commit v1 on v0

v1 whole, which is shorter than its diff:
```python
import functools

import jax
import jax.numpy as jnp
from jax import lax
from jax.experimental import pallas as pl
from jax.experimental.pallas import tpu as pltpu
from jax.sharding import PartitionSpec as P

EPS = 1e-6
HEAD = 128
MESH = pl.DeviceIdType.MESH
F32 = jnp.float32
BF16 = jnp.bfloat16
VMEM_LIMIT = 67043328
NC = 4
MAIN = 32
OVER = 4
CB = 256


def rms(x, g):
    xf = x.astype(F32)
    return (xf * lax.rsqrt(jnp.mean(xf * xf, axis=-1, keepdims=True) + EPS) * g).astype(BF16)


def dot(a, b):
    return jnp.dot(a, b, preferred_element_type=F32)


def attn_kernel(nseq, x_ref, g1_ref, g2_ref, wq_ref, wk_ref, wv_ref, wo_ref, h_ref, z_ref, xn, o_buf, acc):
    i = pl.program_id(0)
    s_len = x_ref.shape[0] // nseq

    @pl.when(i == 0)
    def _():
        xn[...] = rms(x_ref[...], g1_ref[...])
        acc[...] = jnp.zeros_like(acc)

    a = xn[...]
    q = dot(a, wq_ref[...]).astype(BF16)
    k = dot(a, wk_ref[...]).astype(BF16)
    v = dot(a, wv_ref[...]).astype(BF16)
    row = lax.broadcasted_iota(jnp.int32, (s_len, s_len), 0)
    col = lax.broadcasted_iota(jnp.int32, (s_len, s_len), 1)
    mask = row >= col
    for s in range(nseq):
        for hd in range(wq_ref.shape[1] // HEAD):
            r = slice(s * s_len, (s + 1) * s_len)
            c = slice(hd * HEAD, (hd + 1) * HEAD)
            sc = lax.dot_general(q[r, c], k[r, c], (((1,), (1,)), ((), ())), preferred_element_type=F32) * HEAD ** -0.5
            sc = jnp.where(mask, sc, -1e30)
            e = jnp.exp(sc - jnp.max(sc, axis=-1, keepdims=True))
            p = (e / jnp.sum(e, axis=-1, keepdims=True)).astype(BF16)
            o_buf[r, c] = dot(p, v[r, c]).astype(BF16)
    acc[...] += dot(o_buf[...], wo_ref[...])

    @pl.when(i == pl.num_programs(0) - 1)
    def _():
        h = (x_ref[...].astype(F32) + acc[...].astype(BF16).astype(F32)).astype(BF16)
        h_ref[...] = h
        z = rms(h, g2_ref[...])
        w = z_ref.shape[2]
        for c in range(z_ref.shape[0]):
            z_ref[c] = z[:, c * w:(c + 1) * w]


def attention(xf, g1, g2, wq, wk, wv, wo, nseq):
    t, d = xf.shape
    wid = wq.shape[1]
    hb = 256
    full = pl.BlockSpec((t, d), lambda i: (0, 0))
    vec = pl.BlockSpec((1, d), lambda i: (0, 0))
    wspec = pl.BlockSpec((d, hb), lambda i: (0, i))
    return pl.pallas_call(
        functools.partial(attn_kernel, nseq),
        grid=(wid // hb,),
        in_specs=[full, vec, vec, wspec, wspec, wspec, pl.BlockSpec((hb, d), lambda i: (i, 0))],
        out_specs=[full, pl.BlockSpec((NC, t, d // NC), lambda i: (0, 0, 0))],
        out_shape=[jax.ShapeDtypeStruct((t, d), BF16), jax.ShapeDtypeStruct((NC, t, d // NC), BF16)],
        scratch_shapes=[pltpu.VMEM((t, d), BF16), pltpu.VMEM((t, hb), BF16), pltpu.VMEM((t, d), F32)],
        compiler_params=pltpu.CompilerParams(vmem_limit_bytes=VMEM_LIMIT),
        name="attention",
    )(xf, g1.reshape(1, d), g2.reshape(1, d), wq, wk, wv, wo)


def local_ranks(meta, base, n_loc):
    top, t = meta.shape[0] // 2, meta.shape[1]
    e = lax.broadcasted_iota(jnp.int32, (n_loc, t), 0).astype(F32) + base
    m = jnp.zeros((n_loc, t), F32)
    g = jnp.zeros((n_loc, t), F32)
    for j in range(top):
        hit = meta[j:j + 1, :] == e
        m = m + jnp.where(hit, 1.0, 0.0)
        g = g + jnp.where(hit, meta[top + j:top + j + 1, :], 0.0)
    before = lax.broadcasted_iota(jnp.int32, (t, t), 0) < lax.broadcasted_iota(jnp.int32, (t, t), 1)
    rank = dot(m.astype(BF16), jnp.where(before, 1.0, 0.0).astype(BF16))
    return jnp.where(m > 0.5, rank, 255.0).astype(BF16), g


def slot_of(q, src, n_loc):
    main = n_loc * MAIN
    is_main = q < main
    qo = q - main
    ko = qo % (4 * OVER)
    exp = jnp.where(is_main, q // MAIN, qo // (4 * OVER))
    rank = jnp.where(is_main, q % MAIN, jnp.where(ko // OVER == src % 4, MAIN + ko % OVER, -1))
    return exp, rank


def up_kernel(n_loc, z_ref, meta_ref, w1_ref, w3_ref, u_ref, gm_ref,
              zr, ss, xbuf, acc, wbuf, ubuf, zsem, wsem, usem, m_send, m_recv, ssem, rsem):
    ep = lax.axis_size("ep")
    me = lax.axis_index("ep")
    core = lax.rem(me, 2)
    chip = lax.div(me, 2)
    nch = ep // 2
    other = me + 1 - 2 * core

    def dev(ch, co):
        return 2 * lax.rem(ch + nch, nch) + co

    right, left, far = dev(chip + 1, core), dev(chip - 1, core), dev(chip + 2, core)
    orig, olef, ofar, own_o = dev(chip + 1, 1 - core), dev(chip - 1, 1 - core), dev(chip + 2, 1 - core), other
    t, ck = zr.shape[2], zr.shape[3]
    half = t // 2
    ff = w1_ref.shape[2]
    W = wbuf.shape[0]

    def zload(k):
        return pltpu.make_async_copy(z_ref.at[k], zr.at[k, me], zsem.at[k])

    for k in range(NC):
        zload(k).start()

    def wload(i):
        slot = lax.rem(i, W)
        e = lax.rem(i, n_loc)
        k0 = pl.multiple_of(lax.div(i, n_loc) * ck, ck)
        return (pltpu.make_async_copy(w1_ref.at[e, pl.ds(k0, ck), :], wbuf.at[slot, 0], wsem.at[slot, 0]),
                pltpu.make_async_copy(w3_ref.at[e, pl.ds(k0, ck), :], wbuf.at[slot, 1], wsem.at[slot, 1]))

    for i in range(W - 1):
        for c in wload(i):
            c.start()

    barrier = pltpu.get_barrier_semaphore()
    for off in range(1, 8):
        pl.semaphore_signal(barrier, inc=1, device_id={"ep": lax.rem(me + off, ep)}, device_id_type=MESH)
    pl.semaphore_wait(barrier, 7)

    def mcopy(off, slot):
        return pltpu.make_async_remote_copy(meta_ref, gm_ref.at[slot], m_send.at[off - 1], m_recv.at[off - 1],
                                            device_id={"ep": lax.rem(me + off, ep)}, device_id_type=MESH)

    for off in range(1, 8):
        mcopy(off, me).start()

    lo, hi, al = pl.ds(0, half), pl.ds(half, half), pl.ds(0, t)

    def rc(kind, k, src, rows, to):
        ref = zr.at[k, src, rows]
        return pltpu.make_async_remote_copy(ref, ref, ssem.at[kind, k], rsem.at[kind, k],
                                            device_id={"ep": to}, device_id_type=MESH)

    def sends(k):
        return {
            0: rc(0, k, me, lo, right), 1: rc(1, k, me, hi, right),
            2: rc(2, k, me, hi, left), 3: rc(3, k, me, lo, left),
            4: rc(4, k, left, lo, right), 5: rc(5, k, right, hi, left),
            6: rc(6, k, me, al, other), 7: rc(7, k, left, al, other), 8: rc(8, k, right, al, other),
            9: rc(9, k, far, lo, other), 10: rc(10, k, far, hi, other),
        }

    def recvs(k):
        return {
            0: rc(0, k, left, lo, right), 1: rc(1, k, left, hi, right),
            2: rc(2, k, right, hi, left), 3: rc(3, k, right, lo, left),
            4: rc(4, k, far, lo, right), 5: rc(5, k, far, hi, left),
            6: rc(6, k, own_o, al, other), 7: rc(7, k, olef, al, other), 8: rc(8, k, orig, al, other),
            9: rc(9, k, ofar, lo, other), 10: rc(10, k, ofar, hi, other),
        }

    S = [sends(k) for k in range(NC)]
    R = [recvs(k) for k in range(NC)]

    def own(k):
        zload(k).wait()
        for kind in (0, 2, 1, 3, 6):
            S[k][kind].start()

    def poll_a(k):
        R[k][0].wait_recv()
        S[k][4].start()
        R[k][2].wait_recv()
        S[k][5].start()
        if k + 1 < NC:
            own(k + 1)

    def poll_b(k):
        R[k][1].wait_recv()
        S[k][7].start()
        R[k][3].wait_recv()
        S[k][8].start()

    def poll_c(k):
        R[k][4].wait_recv()
        S[k][9].start()
        R[k][5].wait_recv()
        S[k][10].start()
        for kind in (6, 7, 8, 9, 10):
            R[k][kind].wait_recv()

    own(0)
    gm_ref[me] = meta_ref[...]
    for off in range(1, 8):
        mcopy(off, lax.rem(me - off + ep, ep)).wait_recv()
    base = (me * n_loc).astype(F32)

    rows = ss.shape[1]

    def build(s, _):
        rank, _g = local_ranks(gm_ref[s], base, n_loc)
        q1 = lax.broadcasted_iota(jnp.int32, (rows, n_loc), 0)
        e1 = lax.broadcasted_iota(jnp.int32, (rows, n_loc), 1)
        ex = jnp.where(slot_of(q1, s, n_loc)[0] == e1, 1.0, 0.0).astype(BF16)
        r = dot(ex, rank)
        want = slot_of(lax.broadcasted_iota(jnp.int32, (rows, t), 0), s, n_loc)[1].astype(F32)
        ss[s] = jnp.where(r == want, 1.0, 0.0).astype(BF16)
        return 0

    lax.fori_loop(0, 4, build, 0)
    poll_a(0)
    lax.fori_loop(4, 8, build, 0)
    poll_b(0)
    poll_c(0)

    main = n_loc * MAIN

    def expert(k, e, _):
        i = k * n_loc + e
        slot = lax.rem(i, W)

        @pl.when(i + W - 1 < NC * n_loc)
        def _():
            for c in wload(i + W - 1):
                c.start()

        for c in wload(i):
            c.wait()
        x = xbuf[e]
        h1 = dot(x, wbuf[slot, 0])
        h3 = dot(x, wbuf[slot, 1])
        if k == 0:
            acc[e, 0] = h1
            acc[e, 1] = h3
        elif k < NC - 1:
            acc[e, 0] += h1
            acc[e, 1] += h3
        else:
            us = lax.rem(e, 2)

            @pl.when(e >= 2)
            def _():
                pltpu.make_async_copy(ubuf.at[us], u_ref.at[e - 2], usem.at[us]).wait()

            h1 = acc[e, 0] + h1
            h3 = acc[e, 1] + h3
            ubuf[us] = (h1 * jax.nn.sigmoid(h1) * h3).astype(BF16)
            pltpu.make_async_copy(ubuf.at[us], u_ref.at[e], usem.at[us]).start()
        return 0

    for k in range(NC):
        for hf in range(2):
            over = None
            for s4 in range(4):
                s = 4 * hf + s4
                g = dot(ss[s], zr[k, s])
                xbuf[:, s * MAIN:(s + 1) * MAIN, :] = g[:main].astype(BF16).reshape(n_loc, MAIN, ck)
                over = g[main:] if over is None else over + g[main:]
            o0 = 8 * MAIN + hf * 4 * OVER
            xbuf[:, o0:o0 + 4 * OVER, :] = over.astype(BF16).reshape(n_loc, 4 * OVER, ck)
        body = functools.partial(expert, k)
        if k + 1 < NC:
            lax.fori_loop(0, 4, body, 0)
            poll_a(k + 1)
            lax.fori_loop(4, 10, body, 0)
            poll_b(k + 1)
            lax.fori_loop(10, n_loc, body, 0)
            poll_c(k + 1)
        else:
            lax.fori_loop(0, n_loc, body, 0)

    for e in (n_loc - 2, n_loc - 1):
        pltpu.make_async_copy(ubuf.at[e % 2], u_ref.at[e], usem.at[e % 2]).wait()
    for off in range(1, 8):
        mcopy(off, me).wait_send()
    for k in range(NC):
        for kind in range(11):
            S[k][kind].wait_send()


def gather_up(z, meta, w1, w3):
    n_loc, d, ff = w1.shape
    nc, t, ck = z.shape
    rows = n_loc * (MAIN + 4 * OVER)
    per = 8 * MAIN + 8 * OVER
    wslots = 4
    anys = pl.BlockSpec(memory_space=pl.ANY)
    vm = pl.BlockSpec(memory_space=pltpu.VMEM)
    return pl.pallas_call(
        functools.partial(up_kernel, n_loc),
        in_specs=[anys, vm, anys, anys],
        out_specs=[anys, vm],
        out_shape=[jax.ShapeDtypeStruct((n_loc, per, ff), BF16), jax.ShapeDtypeStruct((8,) + meta.shape, F32)],
        scratch_shapes=[
            pltpu.VMEM((nc, 8, t, ck), BF16),
            pltpu.VMEM((8, rows, t), BF16),
            pltpu.VMEM((n_loc, per, ck), BF16),
            pltpu.VMEM((n_loc, 2, per, ff), F32),
            pltpu.VMEM((wslots, 2, ck, ff), BF16),
            pltpu.VMEM((2, per, ff), BF16),
            pltpu.SemaphoreType.DMA((nc,)),
            pltpu.SemaphoreType.DMA((wslots, 2)),
            pltpu.SemaphoreType.DMA((2,)),
            pltpu.SemaphoreType.DMA((7,)),
            pltpu.SemaphoreType.DMA((7,)),
            pltpu.SemaphoreType.DMA((11, nc)),
            pltpu.SemaphoreType.DMA((11, nc)),
        ],
        compiler_params=pltpu.CompilerParams(vmem_limit_bytes=VMEM_LIMIT, collective_id=0, has_side_effects=True),
        name="gather_up",
    )(z, meta, w1, w3)


def down_kernel(n_loc, u_ref, gm_ref, w2_ref, h_ref, y_ref,
                ub, gg, ecat, wbuf, pbuf, qbuf, tbuf, drecv, xrecv, usem, wsem, dss, drs, xss, xrs):
    ep = lax.axis_size("ep")
    me = lax.axis_index("ep")
    core = lax.rem(me, 2)
    chip = lax.div(me, 2)
    nch = ep // 2
    other = me + 1 - 2 * core
    t = h_ref.shape[0]
    ncb = h_ref.shape[1] // CB
    W = wbuf.shape[0]
    main = n_loc * MAIN
    rows = n_loc * (MAIN + 4 * OVER)
    hc = CB // 2

    def dev(ch, co):
        return 2 * lax.rem(ch + nch, nch) + co

    right, left = dev(chip + 1, core), dev(chip - 1, core)

    ucopy = pltpu.make_async_copy(u_ref, ub, usem)
    ucopy.start()

    def wload(i):
        slot = lax.rem(i, W)
        e = lax.rem(i, n_loc)
        c0 = pl.multiple_of(lax.div(i, n_loc) * CB, CB)
        return pltpu.make_async_copy(w2_ref.at[e, :, pl.ds(c0, CB)], wbuf.at[slot], wsem.at[slot])

    for i in range(W - 1):
        wload(i).start()

    barrier = pltpu.get_barrier_semaphore()
    for peer in (right, left, other):
        pl.semaphore_signal(barrier, inc=1, device_id={"ep": peer}, device_id_type=MESH)
    pl.semaphore_wait(barrier, 3)

    base = (me * n_loc).astype(F32)

    def build(s, _):
        rank, g = local_ranks(gm_ref[s], base, n_loc)
        g_hi = g.astype(BF16)
        r1 = g - g_hi.astype(F32)
        g_mid = r1.astype(BF16)
        g_lo = (r1 - g_mid.astype(F32)).astype(BF16)
        e1 = lax.broadcasted_iota(jnp.int32, (n_loc, rows), 0)
        q1 = lax.broadcasted_iota(jnp.int32, (n_loc, rows), 1)
        ex = jnp.where(slot_of(q1, s, n_loc)[0] == e1, 1.0, 0.0).astype(BF16)
        want = slot_of(lax.broadcasted_iota(jnp.int32, (t, rows), 1), s, n_loc)[1].astype(F32)

        def expand(a):
            return lax.dot_general(a, ex, (((0,), (0,)), ((), ())), preferred_element_type=F32)

        keep = expand(rank) == want
        for n, part in enumerate((g_hi, g_mid, g_lo)):
            gg[s, :, n * rows:(n + 1) * rows] = jnp.where(keep, expand(part), 0.0).astype(BF16)
        return 0

    lax.fori_loop(0, 8, build, 0)
    ucopy.wait()

    def partial(s):
        e = ecat[s]
        return (dot(gg[s, :, 0:rows], e) + dot(gg[s, :, rows:2 * rows], e)) + dot(gg[s, :, 2 * rows:3 * rows], e)

    def dst(j):
        return lax.rem(chip + jnp.where(j == 0, 2, jnp.where(j == 1, 1, jnp.where(j == 2, 3, 0))), nch)

    def dcopy(n, j):
        sl = lax.rem(n, 2)
        return pltpu.make_async_remote_copy(pbuf.at[sl, j], drecv.at[n, j], dss.at[sl, j], drs.at[n, j],
                                            device_id={"ep": other}, device_id_type=MESH)

    def xcopy(n, kind):
        sl = lax.rem(n, 3)
        src = {0: qbuf.at[sl, 0, 0], 1: qbuf.at[sl, 0, 1], 2: qbuf.at[sl, 1, 0], 3: qbuf.at[sl, 2, 1],
               4: tbuf.at[lax.rem(n, 2), 0], 5: tbuf.at[lax.rem(n, 2), 1]}[kind]
        to = left if kind in (0, 3, 4) else right
        ssl = sl if kind < 4 else lax.rem(n, 2)
        return pltpu.make_async_remote_copy(src, xrecv.at[n, kind], xss.at[kind, ssl], xrs.at[n, kind],
                                            device_id={"ep": to}, device_id_type=MESH)

    def stage_a(n):
        sl = lax.rem(n, 2)
        sq = lax.rem(n, 3)

        def expert(e, _):
            i = n * n_loc + e

            @pl.when(i + W - 1 < ncb * n_loc)
            def _():
                wload(i + W - 1).start()

            wload(i).wait()
            o = dot(ub[e], wbuf[lax.rem(i, W)]).astype(BF16)
            r0 = pl.multiple_of(e * MAIN, MAIN)
            r1 = pl.multiple_of(main + e * 4 * OVER, 4 * OVER)
            for s in range(8):
                ecat[s, pl.ds(r0, MAIN), :] = o[s * MAIN:(s + 1) * MAIN]
                b = 8 * MAIN + (s // 4) * 4 * OVER
                ecat[s, pl.ds(r1, 4 * OVER), :] = o[b:b + 4 * OVER]
            return 0

        lax.fori_loop(0, n_loc, expert, 0)

        def theirs(j, _):
            @pl.when(n >= 2)
            def _():
                dcopy(n - 2, j).wait_send()

            pbuf[sl, j] = partial(2 * dst(j) + 1 - core)
            dcopy(n, j).start()
            return 0

        lax.fori_loop(0, 4, theirs, 0)

        @pl.when(n >= 3)
        def _():
            for kind in range(4):
                xcopy(n - 3, kind).wait_send()

        def ours(j, _):
            p = partial(2 * dst(j) + core)
            dcopy(n, j).wait_recv()
            p = p + drecv[n, j]
            qbuf[sq, j, 0] = p[:, :hc]
            qbuf[sq, j, 1] = p[:, hc:]

            @pl.when(j == 0)
            def _():
                xcopy(n, 0).start()
                xcopy(n, 1).start()

            @pl.when(j == 1)
            def _():
                xcopy(n, 2).start()

            @pl.when(j == 2)
            def _():
                xcopy(n, 3).start()

            return 0

        lax.fori_loop(0, 4, ours, 0)

    def stage_c(n):
        sq = lax.rem(n, 3)
        st = lax.rem(n, 2)

        @pl.when(n >= 2)
        def _():
            xcopy(n - 2, 4).wait_send()
            xcopy(n - 2, 5).wait_send()

        xcopy(n, 0).wait_recv()
        tbuf[st, 0] = qbuf[sq, 2, 0] + xrecv[n, 0]
        xcopy(n, 4).start()
        xcopy(n, 1).wait_recv()
        tbuf[st, 1] = qbuf[sq, 1, 1] + xrecv[n, 1]
        xcopy(n, 5).start()

    def stage_d(n):
        sq = lax.rem(n, 3)
        for kind in (2, 3, 4, 5):
            xcopy(n, kind).wait_recv()
        c0 = pl.multiple_of(n * CB, CB)
        a = (qbuf[sq, 3, 0] + xrecv[n, 2]) + xrecv[n, 4]
        b = (qbuf[sq, 3, 1] + xrecv[n, 3]) + xrecv[n, 5]
        y_ref[:, pl.ds(c0, hc)] = (h_ref[:, pl.ds(c0, hc)].astype(F32) + a).astype(BF16)
        y_ref[:, pl.ds(c0 + hc, hc)] = (h_ref[:, pl.ds(c0 + hc, hc)].astype(F32) + b).astype(BF16)

    def step(n, _):
        @pl.when(n < ncb)
        def _():
            stage_a(n)

        @pl.when(jnp.logical_and(n >= 1, n - 1 < ncb))
        def _():
            stage_c(n - 1)

        @pl.when(n >= 2)
        def _():
            stage_d(n - 2)

        return 0

    lax.fori_loop(0, ncb + 2, step, 0)

    for n in (ncb - 2, ncb - 1):
        for j in range(4):
            dcopy(n, j).wait_send()
        for kind in (4, 5):
            xcopy(n, kind).wait_send()
    for n in (ncb - 3, ncb - 2, ncb - 1):
        for kind in range(4):
            xcopy(n, kind).wait_send()


def down_reduce(u, gm, w2, h):
    n_loc, ff, d = w2.shape
    t = h.shape[0]
    ncb = d // CB
    rows = n_loc * (MAIN + 4 * OVER)
    wslots = 6
    anys = pl.BlockSpec(memory_space=pl.ANY)
    vm = pl.BlockSpec(memory_space=pltpu.VMEM)
    return pl.pallas_call(
        functools.partial(down_kernel, n_loc),
        in_specs=[anys, vm, anys, vm],
        out_specs=vm,
        out_shape=jax.ShapeDtypeStruct((t, d), BF16),
        scratch_shapes=[
            pltpu.VMEM(u.shape, BF16),
            pltpu.VMEM((8, t, 3 * rows), BF16),
            pltpu.VMEM((8, rows, CB), BF16),
            pltpu.VMEM((wslots, ff, CB), BF16),
            pltpu.VMEM((2, 4, t, CB), F32),
            pltpu.VMEM((3, 4, 2, t, CB // 2), F32),
            pltpu.VMEM((2, 2, t, CB // 2), F32),
            pltpu.VMEM((ncb, 4, t, CB), F32),
            pltpu.VMEM((ncb, 6, t, CB // 2), F32),
            pltpu.SemaphoreType.DMA,
            pltpu.SemaphoreType.DMA((wslots,)),
            pltpu.SemaphoreType.DMA((2, 4)),
            pltpu.SemaphoreType.DMA((ncb, 4)),
            pltpu.SemaphoreType.DMA((6, 3)),
            pltpu.SemaphoreType.DMA((ncb, 6)),
        ],
        compiler_params=pltpu.CompilerParams(vmem_limit_bytes=VMEM_LIMIT, collective_id=1, has_side_effects=True),
        name="down_reduce",
    )(u, gm, w2, h)


def solution(mesh):
    tok = P(('dp', 'ep'))
    rep = P()
    exs = P('ep')

    def body(x, idx, gates, g1, wq, wk, wv, wo, g2, w1, w3, w2):
        n, s_len, d = x.shape
        t = n * s_len
        top = idx.shape[-1]
        meta = jnp.concatenate([idx.reshape(t, top).T.astype(F32), gates.reshape(t, top).T], axis=0)
        h, z = attention(x.reshape(t, d), g1, g2, wq, wk, wv, wo, n)
        u, gm = gather_up(z, meta, w1, w3)
        y = down_reduce(u, gm, w2, h)
        return y.reshape(n, s_len, d)

    return jax.shard_map(body, mesh=mesh, in_specs=(tok, tok, tok, rep, rep, rep, rep, rep, rep, exs, exs, exs), out_specs=tok, check_vma=False)
```

time: 891 us -> 292 us (0.33)
  Pallas kernels: 0 us -> 286 us
  local copies, waits for them, and re-layouts: 231 us -> 2.73 us
  blocking collectives: 212 us -> 0 us
  waiting for transfers between devices: 206 us -> 0 us
  matrix products: 186 us -> 0 us
  other arithmetic: 42.9 us -> 2.01 us
    pallas_call x0 -> x3, Pallas kernels: none -> 286 us  [the longest x1 125 us: down_reduce(): pl.pallas_call(functools.partial(down_kernel, n_loc), in_specs=[anys, vm,...]
    all_to_all x1 -> x0, blocking collectives: 212 us -> none  [body(): recv = lax.all_to_all(buf, 'ep', 0, 0, tiled=True)]
    all_to_all x1 -> x0, waiting for transfers between devices: 206 us -> none  [body(): back = lax.all_to_all(e_out, 'ep', 0, 0, tiled=True)]
    dot_general x13 -> x0, matrix products: 182 us -> none  [the longest x1 53.5 us: body(): h1 = jnp.einsum('gnd,gdf->gnf', r, w1, preferred_element_type=jnp.float32)]
    gather x3 -> x0, local copies, waits for them, and re-layouts: 68.7 us -> none  [the longest x1 32.6 us: body(): got = back[dest].reshape(t, top, d).astype(jnp.float32)]
    scatter x2 -> x0, local copies, waits for them, and re-layouts: 40.5 us -> none  [the longest x1 28.5 us: body(): jnp.zeros((n_exp * cap, d), jnp.bfloat16).at[dest]]
    all_to_all x2 -> x0, local copies, waits for them, and re-layouts: 38.7 us -> none  [the longest x1 26.7 us: body(): recv = lax.all_to_all(buf, 'ep', 0, 0, tiled=True)]
    transpose x2 -> x0, local copies, waits for them, and re-layouts: 37.8 us -> none  [the longest x1 25.8 us: body(): e_out.reshape(g_loc, ep, cap, d).transpose(1, 0, 2, 3)]
  transfers between devices with their start and end apart: 1 -> 0, of which waited for: 1 -> 0; matrix products, arithmetic and copies ran while one was open for 0% -> 0% of each run, Pallas kernels for 0% -> 0%
where the time goes in v1:
time: 292 us; the launch traced here: 291 us
  Pallas kernels  286 us (98%)
    pallas_call x1, Pallas kernels, down_reduce(): pl.pallas_call(functools.partial(down_kernel, n_loc), in_specs=[anys, vm,...  125 us
    pallas_call x1, Pallas kernels, gather_up(): pl.pallas_call(functools.partial(up_kernel, n_loc), in_specs=[anys, vm, a...  88.2 us
    pallas_call x1, Pallas kernels, attention(): pl.pallas_call(functools.partial(attn_kernel, nseq), grid=(wid // hb,), i...  72.6 us

profile of v1, /device:TPU:81, one launch (start us, length us, event | category | flops | bytes accessed | tf_op | source)
XLA Modules:
  0.0 291.1 jit_solution(6888900460070783400)
XLA Ops:
  0.0 0.7 convert_bitcast_fusion
  0.7 1.3 pad_maximum_fusion.meta_ref
  2.0 72.6 %attention.1 = (bf16[384,2048]{1,0:T(8,128)(2,1)}, bf16[4,384,512]{2,1,0:T(8,128)(2,1)}) custom-call(bf16[384,2048]{1,0:T(8,128)(2,1)} %bitcast.12, f32[1,2048]{1,0:T(1,128)} %bitcast.14, f32[1,2048]{1,0:T(1,128)} %bitcast.15, bf16[2048,4096]{1,0:T(8,128)(2,1)} %wq_ref.1, bf16[2048,4096]{1,0:T(8,128)(2,1)} %wk_ref.1, bf16[2048,4096]{1,0:T(8,128)(2,1)} %wv_ref.1, ...), custom_call_target="tpu_custom_call" | custom-call | tf_op jit(solution)/shard_map/attention/pallas_call | solution.py:75
  74.7 88.2 %gather_up.1 = (bf16[16,288,768]{2,1,0:T(8,128)(2,1)}, f32[8,16,384]{2,1,0:T(8,128)}) custom-call(bf16[4,384,512]{2,1,0:T(8,128)(2,1)} %get-tuple-element.9.z_ref, f32[16,384]{1,0:T(8,128)} %pad_maximum_fusion.meta_ref, bf16[16,2048,768]{2,1,0:T(8,128)(2,1)} %w1_ref.1, bf16[16,2048,768]{2,1,0:T(8,128)(2,1)} %w3_ref.1), custom_call_target="tpu_custom_call" | custom-call | tf_op jit(solution)/shard_map/gather_up/pallas_call | solution.py:311
  162.9 125.4 %down_reduce.1 = bf16[384,2048]{1,0:T(8,128)(2,1)} custom-call(bf16[16,288,768]{2,1,0:T(8,128)(2,1)} %get-tuple-element.10.u_ref, f32[8,16,384]{2,1,0:T(8,128)} %get-tuple-element.11.gm_ref, bf16[16,768,2048]{2,1,0:T(8,128)(2,1)} %w2_ref.1, bf16[384,2048]{1,0:T(8,128)(2,1)} %get-tuple-element.12.h_ref), custom_call_target="tpu_custom_call" | custom-call | tf_op jit(solution)/shard_map/down_reduce/pallas_call | solution.py:542
  288.4 2.7 copy.14

commit v2 on v0

v2 whole, which is shorter than its diff:
```python
import functools

import jax
import jax.numpy as jnp
from jax import lax
from jax.experimental import pallas as pl
from jax.experimental.pallas import tpu as pltpu
from jax.sharding import PartitionSpec as P

EPS = 1e-6
HEAD = 128
MESH = pl.DeviceIdType.MESH
F32 = jnp.float32
BF16 = jnp.bfloat16
VMEM_LIMIT = 67043328
HB = 512
CHUNKS = (256, 512, 512, 512, 256)
KB = 256
MAIN = 32
OVER = 4
CB = 256


def rms(x, g):
    xf = x.astype(F32)
    return (xf * lax.rsqrt(jnp.mean(xf * xf, axis=-1, keepdims=True) + EPS) * g).astype(BF16)


def dot(a, b):
    return jnp.dot(a, b, preferred_element_type=F32)


def attn_kernel(nseq, x_ref, idx_ref, gates_ref, g1_ref, g2_ref, wq_ref, wk_ref, wv_ref, wo_ref, h_ref, z_ref, meta_ref, xn, qkv, o_buf, s_buf, p_buf, acc):
    i = pl.program_id(0)
    s_len = x_ref.shape[0] // nseq
    blocks = x_ref.shape[0] // 32

    @pl.when(i == 0)
    def _():
        def ini(b, _):
            r = pl.ds(pl.multiple_of(b * 32, 32), 32)
            xn[r, :] = rms(x_ref[r, :], g1_ref[...])
            acc[r, :] = jnp.zeros((32, acc.shape[1]), F32)
            return 0
        lax.fori_loop(0, blocks, ini, 0)
        top = idx_ref.shape[1]
        for s in range(nseq):
            c = slice(s * s_len, (s + 1) * s_len)
            meta_ref[:top, c] = idx_ref[s].astype(F32)
            meta_ref[top:, c] = gates_ref[s]

    row = lax.broadcasted_iota(jnp.int32, (s_len, s_len), 0)
    col = lax.broadcasted_iota(jnp.int32, (s_len, s_len), 1)
    mask = row >= col
    heads = wq_ref.shape[1] // HEAD
    pairs = [(s * heads + hd, slice(s * s_len, (s + 1) * s_len), slice(hd * HEAD, (hd + 1) * HEAD))
             for s in range(nseq) for hd in range(heads)]

    qkv[0] = dot(xn[...], wq_ref[...]).astype(BF16)
    qkv[1] = dot(xn[...], wk_ref[...]).astype(BF16)
    for n, r, c in pairs:
        sc = lax.dot_general(qkv[0, r, c], qkv[1, r, c], (((1,), (1,)), ((), ())), preferred_element_type=F32)
        s_buf[n] = jnp.where(mask, sc * HEAD ** -0.5, -1e30)
    for n, r, c in pairs:
        sc = s_buf[n]
        e = jnp.exp(sc - jnp.max(sc, axis=-1, keepdims=True))
        p_buf[n] = (e * (1.0 / jnp.sum(e, axis=-1, keepdims=True))).astype(BF16)
    qkv[2] = dot(xn[...], wv_ref[...]).astype(BF16)
    for n, r, c in pairs:
        o_buf[r, c] = dot(p_buf[n], qkv[2, r, c]).astype(BF16)
    acc[...] += dot(o_buf[...], wo_ref[...])

    @pl.when(i == pl.num_programs(0) - 1)
    def _():
        def fin(b, _):
            r = pl.ds(pl.multiple_of(b * 32, 32), 32)
            h = (x_ref[r, :].astype(F32) + acc[r, :].astype(BF16).astype(F32)).astype(BF16)
            h_ref[r, :] = h
            z_ref[r, :] = rms(h, g2_ref[...])
            return 0
        lax.fori_loop(0, blocks, fin, 0)


def attention(xf, idx, gates, g1, g2, wq, wk, wv, wo, nseq):
    t, d = xf.shape
    top = idx.shape[1]
    route = pl.BlockSpec(idx.shape, lambda i: (0, 0, 0))
    wid = wq.shape[1]
    n_pair = nseq * (HB // HEAD)
    s_len = t // nseq
    full = pl.BlockSpec((t, d), lambda i: (0, 0))
    vec = pl.BlockSpec((1, d), lambda i: (0, 0))
    wspec = pl.BlockSpec((d, HB), lambda i: (0, i))
    return pl.pallas_call(
        functools.partial(attn_kernel, nseq),
        grid=(wid // HB,),
        in_specs=[full, route, route, vec, vec, wspec, wspec, wspec, pl.BlockSpec((HB, d), lambda i: (i, 0))],
        out_specs=[full, full, pl.BlockSpec((2 * top, t), lambda i: (0, 0))],
        out_shape=[jax.ShapeDtypeStruct((t, d), BF16), jax.ShapeDtypeStruct((t, d), BF16), jax.ShapeDtypeStruct((2 * top, t), F32)],
        scratch_shapes=[pltpu.VMEM((t, d), BF16), pltpu.VMEM((3, t, HB), BF16), pltpu.VMEM((t, HB), BF16),
                        pltpu.VMEM((n_pair, s_len, s_len), F32), pltpu.VMEM((n_pair, s_len, s_len), BF16), pltpu.VMEM((t, d), F32)],
        compiler_params=pltpu.CompilerParams(vmem_limit_bytes=VMEM_LIMIT),
        name="attention",
    )(xf, idx, gates, g1.reshape(1, d), g2.reshape(1, d), wq, wk, wv, wo)


class Group:
    def __init__(self):
        self.ep = lax.axis_size("ep")
        self.me = lax.axis_index("ep")
        self.core = lax.rem(self.me, 2)
        self.chip = lax.div(self.me, 2)
        self.nch = self.ep // 2
        self.right, self.left, self.far = self.dev(1, 0), self.dev(self.nch - 1, 0), self.dev(2, 0)
        self.other = self.dev(0, 1)
        self.rel = (0, 1, self.nch - 1, 2)

    def dev(self, hop, swap):
        return 2 * lax.rem(self.chip + hop, self.nch) + (1 - self.core if swap else self.core)

    def place(self, p):
        return self.dev(self.rel[p // 2], p % 2)


def local_ranks(meta, base, n_loc):
    top, t = meta.shape[0] // 2, meta.shape[1]
    e = lax.broadcasted_iota(jnp.int32, (n_loc, t), 0).astype(F32) + base
    m = jnp.zeros((n_loc, t), F32)
    g = jnp.zeros((n_loc, t), F32)
    for j in range(top):
        hit = meta[j:j + 1, :] == e
        m = m + jnp.where(hit, 1.0, 0.0)
        g = g + jnp.where(hit, meta[top + j:top + j + 1, :], 0.0)
    before = lax.broadcasted_iota(jnp.int32, (t, t), 0) < lax.broadcasted_iota(jnp.int32, (t, t), 1)
    rank = dot(m.astype(BF16), jnp.where(before, 1.0, 0.0).astype(BF16))
    return jnp.where(m > 0.5, rank, 255.0).astype(BF16), g


def slot_of(q, place, n_loc):
    main = n_loc * MAIN
    is_main = q < main
    qo = q - main
    ko = qo % (4 * OVER)
    exp = jnp.where(is_main, q // MAIN, qo // (4 * OVER))
    rank = jnp.where(is_main, q % MAIN, jnp.where(ko // OVER == place % 4, MAIN + ko % OVER, -1))
    return exp, rank


def up_kernel(n_loc, z_ref, meta_ref, w1_ref, w3_ref, u_ref, gm_ref,
              zr, ss, xbuf, acc, wbuf, ubuf, zsem, wsem, usem, m_send, m_recv, ssem, rsem):
    g = Group()
    me, ep = g.me, g.ep
    t, d = z_ref.shape
    half = t // 2
    ff = w1_ref.shape[2]
    W = wbuf.shape[0]
    nk = len(CHUNKS)
    off = [sum(CHUNKS[:k]) for k in range(nk)]
    rows = ss.shape[1]
    main = n_loc * MAIN
    big_it = n_loc // 2
    small_it = n_loc // 4
    t_first = small_it
    t_last = t_first + (nk - 2) * big_it
    t_all = t_last + small_it

    def zload(k):
        c = pl.ds(off[k], CHUNKS[k])
        return pltpu.make_async_copy(z_ref.at[:, c], zr.at[me, :, c], zsem.at[k])

    for k in range(nk):
        zload(k).start()

    def wload(it, j):
        slot = lax.rem(4 * it + j, W)
        big = jnp.logical_and(it >= t_first, it < t_last)
        bi = it - t_first
        e = jnp.where(big, 2 * lax.rem(bi, big_it) + j // 2, 4 * jnp.where(it < t_first, it, it - t_last) + j)
        r0 = jnp.where(big, KB + lax.div(bi, big_it) * (2 * KB) + (j % 2) * KB, jnp.where(it < t_first, 0, off[-1]))
        r = pl.ds(pl.multiple_of(r0, KB), KB)
        return (pltpu.make_async_copy(w1_ref.at[e, r, :], wbuf.at[slot, 0], wsem.at[slot, 0]),
                pltpu.make_async_copy(w3_ref.at[e, r, :], wbuf.at[slot, 1], wsem.at[slot, 1]))

    ahead = W // 4 - 1
    for i in range(ahead):
        for j in range(4):
            for c in wload(i, j):
                c.start()

    barrier = pltpu.get_barrier_semaphore()
    for o in range(1, 8):
        pl.semaphore_signal(barrier, inc=1, device_id={"ep": lax.rem(me + o, ep)}, device_id_type=MESH)
    pl.semaphore_wait(barrier, 7)

    def mcopy(o, slot):
        return pltpu.make_async_remote_copy(meta_ref, gm_ref.at[slot], m_send.at[o - 1], m_recv.at[o - 1],
                                            device_id={"ep": lax.rem(me + o, ep)}, device_id_type=MESH)

    for o in range(1, 8):
        mcopy(o, me).start()

    lo, hi, al = pl.ds(0, half), pl.ds(half, half), pl.ds(0, t)

    def rc(kind, k, src, part, to):
        ref = zr.at[src, part, pl.ds(off[k], CHUNKS[k])]
        return pltpu.make_async_remote_copy(ref, ref, ssem.at[kind, k], rsem.at[kind, k],
                                            device_id={"ep": to}, device_id_type=MESH)

    ways = (g.right, g.right, g.left, g.left, g.right, g.left) + (g.other,) * 5
    parts = (lo, hi, hi, lo, lo, hi, al, al, al, lo, hi)
    sent = (me,) * 4 + (g.left, g.right, me, g.left, g.right, g.far, g.far)
    got = ((g.left,) * 2 + (g.right,) * 2 + (g.far,) * 2
           + (g.other, g.dev(g.nch - 1, True), g.dev(1, True), g.dev(2, True), g.dev(2, True)))
    KINDS = len(ways)

    def send(kind, k):
        return rc(kind, k, sent[kind], parts[kind], ways[kind])

    def recv(kind, k):
        return rc(kind, k, got[kind], parts[kind], ways[kind])

    def own(k):
        zload(k).wait()
        for kind in (0, 2, 1, 3, 6):
            send(kind, k).start()

    def poll_a(k):
        recv(0, k).wait_recv()
        send(4, k).start()
        recv(2, k).wait_recv()
        send(5, k).start()

    def poll_b(k):
        recv(1, k).wait_recv()
        send(7, k).start()
        recv(3, k).wait_recv()
        send(8, k).start()

    def poll_c(k):
        recv(4, k).wait_recv()
        send(9, k).start()
        recv(5, k).wait_recv()
        send(10, k).start()

    own(0)
    gm_ref[me] = meta_ref[...]
    for o in range(1, 8):
        mcopy(o, lax.rem(me - o + ep, ep)).wait_recv()
    base = (me * n_loc).astype(F32)

    def build(p):
        rank, _g = local_ranks(gm_ref[g.place(p)], base, n_loc)
        for r0 in range(0, rows, 256):
            q1 = lax.broadcasted_iota(jnp.int32, (256, n_loc), 0) + r0
            e1 = lax.broadcasted_iota(jnp.int32, (256, n_loc), 1)
            ex = jnp.where(slot_of(q1, p, n_loc)[0] == e1, 1.0, 0.0).astype(BF16)
            want = slot_of(lax.broadcasted_iota(jnp.int32, (256, t), 0) + r0, p, n_loc)[1].astype(F32)
            ss[p, r0:r0 + 256, :] = jnp.where(dot(ex, rank) == want, 1.0, 0.0).astype(BF16)

    for p in range(4):
        build(p)
    poll_a(0)
    own(1)
    for p in range(4, 8):
        build(p)

    poll_b(0)
    poll_c(0)

    def take(k, p, over):
        ck = CHUNKS[k]
        y = dot(ss[p], zr[g.place(p), :, off[k]:off[k] + ck])
        xbuf[:, p * MAIN:(p + 1) * MAIN, :ck] = y[:main].astype(BF16).reshape(n_loc, MAIN, ck)
        over = y[main:] if p % 4 == 0 else over + y[main:]
        if p % 4 == 3:
            o0 = 8 * MAIN + (p // 4) * 4 * OVER
            xbuf[:, o0:o0 + 4 * OVER, :ck] = over.astype(BF16).reshape(n_loc, 4 * OVER, ck)
        return over

    def gather(k):
        over = None
        for kind in (6, 7, 8):
            recv(kind, k).wait_recv()
        for p in range(6):
            over = take(k, p, over)
        for kind in (9, 10):
            recv(kind, k).wait_recv()
        for p in range(6, 8):
            over = take(k, p, over)

    def ucopy(e):
        us = lax.rem(e, 4)
        return pltpu.make_async_copy(ubuf.at[us], u_ref.at[e], usem.at[us])

    def experts(k, i, _):
        last = k == nk - 1
        big = CHUNKS[k] == 2 * KB
        it = i + (0 if k == 0 else t_last if last else t_first + (k - 1) * big_it)

        @pl.when(it + ahead < t_all)
        def _():
            for j in range(4):
                for c in wload(it + ahead, j):
                    c.start()

        for j in range(4):
            for c in wload(it, j):
                c.wait()
        if last:
            @pl.when(i > 0)
            def _():
                for ee in range(4):
                    ucopy(4 * i - 4 + ee).wait()

        s0 = lax.rem(4 * it, W)
        for ee in range(2 if big else 4):
            e = (2 if big else 4) * i + ee
            for f0 in range(0, ff, 256):
                f = slice(f0, f0 + 256)

                def prod(w):
                    if big:
                        return (dot(xbuf[e, :, :KB], wbuf[s0 + 2 * ee, w, :, f])
                                + dot(xbuf[e, :, KB:], wbuf[s0 + 2 * ee + 1, w, :, f]))
                    return dot(xbuf[e, :, :KB], wbuf[s0 + ee, w, :, f])

                h1, h3 = prod(0), prod(1)
                if k > 0:
                    h1, h3 = acc[e, 0, :, f] + h1, acc[e, 1, :, f] + h3
                if last:
                    ubuf[ee, :, f] = (h1 * jax.nn.sigmoid(h1) * h3).astype(BF16)
                else:
                    acc[e, 0, :, f] = h1
                    acc[e, 1, :, f] = h3
        if last:
            for ee in range(4):
                ucopy(4 * i + ee).start()
        return 0

    for k in range(nk):
        gather(k)
        body = functools.partial(experts, k)
        n_it, pa, pb, pc = (small_it, 0, 2, 3) if k in (0, nk - 1) else (big_it, 1, 3, 6)

        def run(i, _):
            if k + 1 < nk:
                @pl.when(i == pa)
                def _():
                    poll_a(k + 1)
                    if k + 2 < nk:
                        own(k + 2)

                @pl.when(i == pb)
                def _():
                    poll_b(k + 1)

                @pl.when(i == pc)
                def _():
                    poll_c(k + 1)

            return body(i, 0)

        lax.fori_loop(0, n_it, run, 0)

    for e in range(n_loc - small_it, n_loc):
        ucopy(e).wait()
    for o in range(1, 8):
        mcopy(o, me).wait_send()
    for k in range(nk):
        for kind in range(KINDS):
            send(kind, k).wait_send()


def gather_up(z, meta, w1, w3):
    n_loc, d, ff = w1.shape
    t = z.shape[0]
    nk = len(CHUNKS)
    rows = n_loc * (MAIN + 4 * OVER)
    per = 8 * MAIN + 8 * OVER
    wslots = 16
    anys = pl.BlockSpec(memory_space=pl.ANY)
    vm = pl.BlockSpec(memory_space=pltpu.VMEM)
    return pl.pallas_call(
        functools.partial(up_kernel, n_loc),
        in_specs=[anys, vm, anys, anys],
        out_specs=[anys, vm],
        out_shape=[jax.ShapeDtypeStruct((n_loc, per, ff), BF16), jax.ShapeDtypeStruct((8,) + meta.shape, F32)],
        scratch_shapes=[
            pltpu.VMEM((8, t, d), BF16),
            pltpu.VMEM((8, rows, t), BF16),
            pltpu.VMEM((n_loc, per, max(CHUNKS)), BF16),
            pltpu.VMEM((n_loc, 2, per, ff), F32),
            pltpu.VMEM((wslots, 2, KB, ff), BF16),
            pltpu.VMEM((4, per, ff), BF16),
            pltpu.SemaphoreType.DMA((nk,)),
            pltpu.SemaphoreType.DMA((wslots, 2)),
            pltpu.SemaphoreType.DMA((4,)),
            pltpu.SemaphoreType.DMA((7,)),
            pltpu.SemaphoreType.DMA((7,)),
            pltpu.SemaphoreType.DMA((11, nk)),
            pltpu.SemaphoreType.DMA((11, nk)),
        ],
        compiler_params=pltpu.CompilerParams(vmem_limit_bytes=VMEM_LIMIT, collective_id=0, has_side_effects=True),
        name="gather_up",
    )(z, meta, w1, w3)


def down_kernel(n_loc, u_ref, gm_ref, w2_ref, h_ref, y_ref,
                ub, gg, ecat, wbuf, pbuf, qbuf, tbuf, drecv, xrecv, hb, usem, hsem, wsem, dss, drs, xss, xrs):
    g = Group()
    me = g.me
    t = h_ref.shape[0]
    ncb = h_ref.shape[1] // CB
    W = wbuf.shape[0]
    main = n_loc * MAIN
    rows = n_loc * (MAIN + 4 * OVER)
    hc = CB // 2

    def ucopy(i4):
        return pltpu.make_async_copy(u_ref.at[pl.ds(4 * i4, 4)], ub.at[pl.ds(4 * i4, 4)], usem.at[i4])

    for i4 in range(n_loc // 4):
        ucopy(i4).start()
    hcopy = pltpu.make_async_copy(h_ref, hb, hsem)
    hcopy.start()

    def wload(i):
        slot = lax.rem(i, W)
        e = lax.rem(i, n_loc)
        c0 = pl.multiple_of(lax.div(i, n_loc) * CB, CB)
        return pltpu.make_async_copy(w2_ref.at[e, :, pl.ds(c0, CB)], wbuf.at[slot], wsem.at[slot])

    for i in range(W - 4):
        wload(i).start()

    barrier = pltpu.get_barrier_semaphore()
    for peer in (g.right, g.left, g.other):
        pl.semaphore_signal(barrier, inc=1, device_id={"ep": peer}, device_id_type=MESH)
    pl.semaphore_wait(barrier, 3)

    base = (me * n_loc).astype(F32)

    hops = (2, 1, g.nch - 1, 0)
    places = (6, 2, 4, 0)

    def build(j, swap, _):
        p = places[j] + swap
        rank, gate = local_ranks(gm_ref[2 * lax.rem(g.chip + hops[j], g.nch) + g.core + swap * (1 - 2 * g.core)], base, n_loc)
        g_hi = gate.astype(BF16)
        r1 = gate - g_hi.astype(F32)
        g_mid = r1.astype(BF16)
        g_lo = (r1 - g_mid.astype(F32)).astype(BF16)
        for r0 in range(0, rows, 256):
            e1 = lax.broadcasted_iota(jnp.int32, (n_loc, 256), 0)
            q1 = lax.broadcasted_iota(jnp.int32, (n_loc, 256), 1) + r0
            ex = jnp.where(slot_of(q1, p, n_loc)[0] == e1, 1.0, 0.0).astype(BF16)
            want = slot_of(lax.broadcasted_iota(jnp.int32, (t, 256), 1) + r0, p, n_loc)[1].astype(F32)

            def expand(a):
                return lax.dot_general(a, ex, (((0,), (0,)), ((), ())), preferred_element_type=F32)

            keep = expand(rank) == want
            for n, part in enumerate((g_hi, g_mid, g_lo)):
                gg[p, :, n * rows + r0:n * rows + r0 + 256] = jnp.where(keep, expand(part), 0.0).astype(BF16)
        return 0

    lax.fori_loop(0, 2, functools.partial(build, 0), 0)

    def partial(p):
        e = ecat[p]
        return (dot(gg[p, :, 0:rows], e) + dot(gg[p, :, rows:2 * rows], e)) + dot(gg[p, :, 2 * rows:3 * rows], e)

    def dcopy(n, j):
        sl = lax.rem(n, 2)
        return pltpu.make_async_remote_copy(pbuf.at[sl, j], drecv.at[sl, j], dss.at[sl, j], drs.at[n, j],
                                            device_id={"ep": g.other}, device_id_type=MESH)

    def xcopy(n, kind):
        sl = lax.rem(n, 3)
        src = {0: qbuf.at[sl, 0, 0], 1: qbuf.at[sl, 0, 1], 2: qbuf.at[sl, 1, 0], 3: qbuf.at[sl, 2, 1],
               4: tbuf.at[lax.rem(n, 2), 0], 5: tbuf.at[lax.rem(n, 2), 1]}[kind]
        to = g.left if kind in (0, 3, 4) else g.right
        ssl = sl if kind < 4 else lax.rem(n, 2)
        return pltpu.make_async_remote_copy(src, xrecv.at[n, kind], xss.at[kind, ssl], xrs.at[n, kind],
                                            device_id={"ep": to}, device_id_type=MESH)

    def stage_a(n):
        sl = lax.rem(n, 2)
        sq = lax.rem(n, 3)

        def experts(i4, _):
            i = n * n_loc + 4 * i4

            @pl.when(i + W - 4 < ncb * n_loc)
            def _():
                for j in range(4):
                    wload(i + W - 4 + j).start()

            @pl.when(n == 0)
            def _():
                ucopy(i4).wait()

            for j in range(4):
                wload(i + j).wait()
            w0 = lax.rem(i, W)
            for j in range(4):
                o = dot(ub[4 * i4 + j], wbuf[w0 + j]).astype(BF16)
                r0 = pl.multiple_of((4 * i4 + j) * MAIN, MAIN)
                r1 = pl.multiple_of(main + (4 * i4 + j) * 4 * OVER, 4 * OVER)
                for s in range(8):
                    ecat[s, pl.ds(r0, MAIN), :] = o[s * MAIN:(s + 1) * MAIN]
                    b = 8 * MAIN + (s // 4) * 4 * OVER
                    ecat[s, pl.ds(r1, 4 * OVER), :] = o[b:b + 4 * OVER]
            return 0

        lax.fori_loop(0, n_loc // 4, experts, 0)

        @pl.when(n >= 3)
        def _():
            for kind in range(4):
                xcopy(n - 3, kind).wait_send()

        def finish(j):
            dcopy(n, j).wait_recv()
            qbuf[sq, j, 0] += drecv[sl, j, :, :hc]
            qbuf[sq, j, 1] += drecv[sl, j, :, hc:]
            for kind in ((0, 1), (2,), (3,), ())[j]:
                xcopy(n, kind).start()

        for j in range(4):
            if j:
                @pl.when(n == 0)
                def _():
                    lax.fori_loop(0, 2, functools.partial(build, j), 0)

            @pl.when(n >= 2)
            def _():
                dcopy(n - 2, j).wait_send()

            pbuf[sl, j] = partial(places[j] + 1)
            p = partial(places[j])
            qbuf[sq, j, 0] = p[:, :hc]
            qbuf[sq, j, 1] = p[:, hc:]
            dcopy(n, j).start()
            if j:
                finish(j - 1)
        finish(3)

    def stage_c(n):
        sq = lax.rem(n, 3)
        st = lax.rem(n, 2)

        @pl.when(n >= 2)
        def _():
            xcopy(n - 2, 4).wait_send()
            xcopy(n - 2, 5).wait_send()

        xcopy(n, 0).wait_recv()
        tbuf[st, 0] = qbuf[sq, 2, 0] + xrecv[n, 0]
        xcopy(n, 4).start()
        xcopy(n, 1).wait_recv()
        tbuf[st, 1] = qbuf[sq, 1, 1] + xrecv[n, 1]
        xcopy(n, 5).start()

    def stage_d(n):
        sq = lax.rem(n, 3)

        @pl.when(n == 0)
        def _():
            hcopy.wait()

        for kind in (2, 3, 4, 5):
            xcopy(n, kind).wait_recv()
        c0 = pl.multiple_of(n * CB, CB)
        a = (qbuf[sq, 3, 0] + xrecv[n, 2]) + xrecv[n, 4]
        b = (qbuf[sq, 3, 1] + xrecv[n, 3]) + xrecv[n, 5]
        y_ref[:, pl.ds(c0, hc)] = (hb[:, pl.ds(c0, hc)].astype(F32) + a).astype(BF16)
        y_ref[:, pl.ds(c0 + hc, hc)] = (hb[:, pl.ds(c0 + hc, hc)].astype(F32) + b).astype(BF16)

    def step(n, _):
        @pl.when(n < ncb)
        def _():
            stage_a(n)

        @pl.when(jnp.logical_and(n >= 1, n - 1 < ncb))
        def _():
            stage_c(n - 1)

        @pl.when(n >= 2)
        def _():
            stage_d(n - 2)

        return 0

    lax.fori_loop(0, ncb + 2, step, 0)

    for n in (ncb - 2, ncb - 1):
        for j in range(4):
            dcopy(n, j).wait_send()
        for kind in (4, 5):
            xcopy(n, kind).wait_send()
    for n in (ncb - 3, ncb - 2, ncb - 1):
        for kind in range(4):
            xcopy(n, kind).wait_send()


def down_reduce(u, gm, w2, h):
    n_loc, ff, d = w2.shape
    t = h.shape[0]
    ncb = d // CB
    rows = n_loc * (MAIN + 4 * OVER)
    wslots = 16
    anys = pl.BlockSpec(memory_space=pl.ANY)
    vm = pl.BlockSpec(memory_space=pltpu.VMEM)
    return pl.pallas_call(
        functools.partial(down_kernel, n_loc),
        in_specs=[anys, vm, anys, anys],
        out_specs=vm,
        out_shape=jax.ShapeDtypeStruct((t, d), BF16),
        scratch_shapes=[
            pltpu.VMEM(u.shape, BF16),
            pltpu.VMEM((8, t, 3 * rows), BF16),
            pltpu.VMEM((8, rows, CB), BF16),
            pltpu.VMEM((wslots, ff, CB), BF16),
            pltpu.VMEM((2, 4, t, CB), F32),
            pltpu.VMEM((3, 4, 2, t, CB // 2), F32),
            pltpu.VMEM((2, 2, t, CB // 2), F32),
            pltpu.VMEM((2, 4, t, CB), F32),
            pltpu.VMEM((ncb, 6, t, CB // 2), F32),
            pltpu.VMEM((t, d), BF16),
            pltpu.SemaphoreType.DMA((n_loc // 4,)),
            pltpu.SemaphoreType.DMA,
            pltpu.SemaphoreType.DMA((wslots,)),
            pltpu.SemaphoreType.DMA((2, 4)),
            pltpu.SemaphoreType.DMA((ncb, 4)),
            pltpu.SemaphoreType.DMA((6, 3)),
            pltpu.SemaphoreType.DMA((ncb, 6)),
        ],
        compiler_params=pltpu.CompilerParams(vmem_limit_bytes=VMEM_LIMIT, collective_id=1, has_side_effects=True),
        name="down_reduce",
    )(u, gm, w2, h)


def solution(mesh):
    tok = P(('dp', 'ep'))
    rep = P()
    exs = P('ep')

    def body(x, idx, gates, g1, wq, wk, wv, wo, g2, w1, w3, w2):
        n, s_len, d = x.shape
        t = n * s_len
        h, z, meta = attention(x.reshape(t, d), idx.transpose(0, 2, 1), gates.transpose(0, 2, 1), g1, g2, wq, wk, wv, wo, n)
        u, gm = gather_up(z, meta, w1, w3)
        y = down_reduce(u, gm, w2, h)
        return y.reshape(n, s_len, d)

    return jax.shard_map(body, mesh=mesh, in_specs=(tok, tok, tok, rep, rep, rep, rep, rep, rep, exs, exs, exs), out_specs=tok, check_vma=False)
```

time: 891 us -> 253 us (0.28)
  Pallas kernels: 0 us -> 250 us
  local copies, waits for them, and re-layouts: 231 us -> 2.73 us
  blocking collectives: 212 us -> 0 us
  waiting for transfers between devices: 206 us -> 0 us
  matrix products: 186 us -> 0 us
  other arithmetic: 42.9 us -> 0 us
    pallas_call x0 -> x3, Pallas kernels: none -> 250 us  [the longest x1 124 us: down_reduce(): pl.pallas_call(functools.partial(down_kernel, n_loc), in_specs=[anys, vm,...]
    all_to_all x1 -> x0, blocking collectives: 212 us -> none  [body(): recv = lax.all_to_all(buf, 'ep', 0, 0, tiled=True)]
    all_to_all x1 -> x0, waiting for transfers between devices: 206 us -> none  [body(): back = lax.all_to_all(e_out, 'ep', 0, 0, tiled=True)]
    dot_general x13 -> x0, matrix products: 182 us -> none  [the longest x1 53.5 us: body(): h1 = jnp.einsum('gnd,gdf->gnf', r, w1, preferred_element_type=jnp.float32)]
    gather x3 -> x0, local copies, waits for them, and re-layouts: 68.7 us -> none  [the longest x1 32.6 us: body(): got = back[dest].reshape(t, top, d).astype(jnp.float32)]
    scatter x2 -> x0, local copies, waits for them, and re-layouts: 40.5 us -> none  [the longest x1 28.5 us: body(): jnp.zeros((n_exp * cap, d), jnp.bfloat16).at[dest]]
    all_to_all x2 -> x0, local copies, waits for them, and re-layouts: 38.7 us -> none  [the longest x1 26.7 us: body(): recv = lax.all_to_all(buf, 'ep', 0, 0, tiled=True)]
    transpose x2 -> x0, local copies, waits for them, and re-layouts: 37.8 us -> none  [the longest x1 25.8 us: body(): e_out.reshape(g_loc, ep, cap, d).transpose(1, 0, 2, 3)]
  transfers between devices with their start and end apart: 1 -> 0, of which waited for: 1 -> 0; matrix products, arithmetic and copies ran while one was open for 0% -> 0% of each run, Pallas kernels for 0% -> 0%
where the time goes in v2:
time: 253 us
  Pallas kernels  250 us (99%)
  local copies, waits for them, and re-layouts  2.73 us (1%)
    pallas_call x1, Pallas kernels, down_reduce(): pl.pallas_call(functools.partial(down_kernel, n_loc), in_specs=[anys, vm,...  124 us
    pallas_call x1, Pallas kernels, gather_up(): pl.pallas_call(functools.partial(up_kernel, n_loc), in_specs=[anys, vm, a...  83.3 us
    pallas_call x1, Pallas kernels, attention(): pl.pallas_call(functools.partial(attn_kernel, nseq), grid=(wid // HB,), i...  42.6 us

profile of v2, /device:TPU:81, one launch (start us, length us, event | category | flops | bytes accessed | tf_op | source)
XLA Modules:
  0.0 252.9 jit_solution(12264805550145488535)
XLA Ops:
  0.0 42.6 %attention.1 = (bf16[384,2048]{1,0:T(8,128)(2,1)}, bf16[384,2048]{1,0:T(8,128)(2,1)}, f32[16,384]{1,0:T(8,128)}) custom-call(bf16[384,2048]{1,0:T(8,128)(2,1)} %bitcast.7, s32[3,8,128]{2,1,0:T(8,128)} %bitcast.8, f32[3,8,128]{2,1,0:T(8,128)} %bitcast.9, f32[1,2048]{1,0:T(1,128)} %bitcast.10, f32[1,2048]{1,0:T(1,128)} %bitcast.11, bf16[2048,4096]{1,0:T(8,128)(2,1)} %wq_ref.1, ...), custom_call_target="tpu_custom_call" | custom-call | tf_op jit(solution)/shard_map/attention/pallas_call | solution.py:94
  42.6 83.3 %gather_up.1 = (bf16[16,288,768]{2,1,0:T(8,128)(2,1)}, f32[8,16,384]{2,1,0:T(8,128)}) custom-call(bf16[384,2048]{1,0:T(8,128)(2,1)} %get-tuple-element.10.z_ref, f32[16,384]{1,0:T(8,128)} %get-tuple-element.11.meta_ref, bf16[16,2048,768]{2,1,0:T(8,128)(2,1)} %w1_ref.1, bf16[16,2048,768]{2,1,0:T(8,128)(2,1)} %w3_ref.1), custom_call_target="tpu_custom_call" | custom-call | tf_op jit(solution)/shard_map/gather_up/pallas_call | solution.py:383
  125.9 124.3 %down_reduce.1 = bf16[384,2048]{1,0:T(8,128)(2,1)} custom-call(bf16[16,288,768]{2,1,0:T(8,128)(2,1)} %get-tuple-element.12.u_ref, f32[8,16,384]{2,1,0:T(8,128)} %get-tuple-element.13.gm_ref, bf16[16,768,2048]{2,1,0:T(8,128)(2,1)} %w2_ref.1, bf16[384,2048]{1,0:T(8,128)(2,1)} %get-tuple-element.14.h_ref), custom_call_target="tpu_custom_call" | custom-call | tf_op jit(solution)/shard_map/down_reduce/pallas_call | solution.py:615
  250.2 2.7 %copy.14 = bf16[3,128,2048]{2,1,0:T(8,128)(2,1)} copy(bf16[3,128,2048]{2,1,0:T(8,128)(2,1)} %bitcast.6) | data formatting | bytes 3145728
